TPU v7x, 256 devices: a whole 4x4x8 slice. The times are simulated.
256 devices in a mesh: blk: 16 (over x_lo, y, core), walk: 16 (over x_hi, z).
Axes of the slice: x: 4 (x_hi: 2, x_lo: 2; x = x_hi * 2 + x_lo), y: 4, z: 8, core: 2. Of those that a mesh axis runs over, the one named last changes fastest.
Arguments:
- walkers: bfloat16 [512, 200, 2048], P(('blk', 'walk')), may hold values from -6 to 6
- inv_intersection: bfloat16 [512, 2, 100, 100], P(('blk', 'walk')), may hold values from -0.625 to 0.625
- rotated_chol: bfloat16 [32, 100, 2048], P('blk'), may hold values from -0.013671875 to 0.013671875
- full_chol: bfloat16 [32, 2048, 2048], P('walk', 'blk'), may hold values from -0.125 to 0.125
- field_noise: float32 [32], replicated, may hold values from -4 to 4
Outputs:
- propagated: bfloat16 [512, 200, 2048], P(('blk', 'walk'))
- force_bias: float32 [512, 32], P(('blk', 'walk'))
- bias_shift: float32 [32], replicated
All inputs are finite; a program needn't handle non-finite values.
Results may differ from a plain program's by a relative error of at most 0.0065.
Values may be sent and summed in bfloat16 or wider, within the bound.
No kernel may reach another device: no remote copies, remote signals or barrier semaphores. Data moves between devices by JAX's collectives and lax.ppermute only.
A program may use at most 128 MiB of HBM per device.

v0:
```python
import functools
import math
import jax
import jax.numpy as jnp
from jax import lax
from jax.sharding import Mesh
from jax.sharding import PartitionSpec as P

BLK = ("blk_0", "blk_1", "blk_2")
WALK = ("walk_0", "walk_1")
BLK_WALK = ("blk_0", "blk_1", "blk_2", "walk_0", "walk_1")
time_root = 0.1


def by_axis(array, axes):
    return functools.reduce(lax.psum, axes, array)


def in_blocks(array, dim, count):
    before, after = (array.shape[:dim], array.shape[dim + 1 :])
    return jnp.moveaxis(array.reshape(*before, count, -1, *after), dim, 0)


def sent_and_summed(array, axis, dim):
    blocks = in_blocks(array, dim, lax.axis_size(axis))
    arrived = lax.all_to_all(blocks, axis, split_axis=0, concat_axis=0, tiled=True)
    return arrived.sum(axis=0)


def sent_to_all(array, axis):
    count = lax.axis_size(axis)
    return lax.all_to_all(
        jnp.broadcast_to(array[None], (count, *array.shape)), axis, 0, 0, tiled=True
    )


def in_order(blocks, dim):
    blocks = jnp.moveaxis(blocks, 0, dim)
    shape = blocks.shape
    return blocks.reshape(*shape[:dim], shape[dim] * shape[dim + 1], *shape[dim + 2 :])


def gather_directly(array, axis, dim):
    blocks = sent_to_all(array, axis)
    return in_order(blocks, dim)


def local(walkers, inv_intersection, rotated_chol, full_chol, field_noise):
    wdev_count, double_rows, orbitals = walkers.shape
    occupied = double_rows // 2
    spins = walkers.reshape(wdev_count, 2, occupied, orbitals)
    theta = jnp.einsum(
        "wsij,wsjp->wip", inv_intersection, spins, preferred_element_type=jnp.float32
    ).astype(jnp.bfloat16)
    flat_theta = theta.reshape(wdev_count, occupied * orbitals)
    piece = lax.all_gather(rotated_chol, BLK, axis=0, tiled=True)
    flat_piece = piece.reshape(piece.shape[0], occupied * orbitals)
    part_bias = lax.dot_general(
        flat_theta, flat_piece, (((1,), (1,)), ((), ())), preferred_element_type=jnp.float32
    )
    total_walkers = wdev_count * lax.axis_size(BLK) * lax.axis_size(WALK)
    bias_shift = by_axis(jnp.sum(part_bias, axis=0), BLK_WALK) / math.sqrt(total_walkers)
    shifted = field_noise - bias_shift
    local_count = full_chol.shape[0]
    local_shift = lax.dynamic_slice_in_dim(shifted, lax.axis_index(WALK) * local_count, local_count)
    partial_value = time_root * jnp.tensordot(
        local_shift, full_chol.astype(jnp.float32), axes=1, precision=lax.Precision.HIGHEST
    )
    narrow = sent_and_summed(partial_value, WALK, 1).astype(jnp.bfloat16)
    row_block = gather_directly(narrow, WALK, 1)
    field = lax.all_gather(row_block, BLK, axis=0, tiled=True)
    current = walkers.reshape(wdev_count * double_rows, orbitals)
    total = current.astype(jnp.float32)
    for order in range(1, 5):
        current = (jnp.dot(current, field, preferred_element_type=jnp.float32) / order).astype(
            jnp.bfloat16
        )
        total = total + current.astype(jnp.float32)
    propagated = total.astype(jnp.bfloat16).reshape(wdev_count, double_rows, orbitals)
    return (propagated, part_bias, bias_shift)


def solution(mesh):
    torus = Mesh(
        mesh.devices.reshape(2, 4, 2, 2, 8), ("blk_0", "blk_1", "blk_2", "walk_0", "walk_1")
    )
    in_specs = (
        P(BLK_WALK, None, None),
        P(BLK_WALK, None, None, None),
        P(BLK, None, None),
        P(WALK, BLK, None),
        P(),
    )
    out_specs = (P(BLK_WALK, None, None), P(BLK_WALK, None), P())
    return jax.shard_map(local, mesh=torus, in_specs=in_specs, out_specs=out_specs, check_vma=False)
```

profile of v0, /device:TPU:1, one launch (start us, length us, event | category | flops | bytes accessed | tf_op | source)
XLA Modules:
  0.0 296.6 jit_solution(11933287155726860161)
XLA Ops:
  7.2 0.0 copy-start
  7.2 0.0 copy-start.2
  7.2 0.0 all-gather.3.cloned.1.call-start
  7.2 2.4 copy.18
  9.6 0.0 all-gather.3.cloned.1.call-update
  9.7 0.0 all-gather.5.cloned.1.call-start
  9.7 1.6 reshape.27
  11.3 0.0 copy-done.2
  11.3 1.4 fusion.6
  12.7 0.0 copy-start.3
  12.7 81.3 %all-gather.3.cloned.1.call-done = bf16[32,100,2048]{2,1,0:T(8,128)(2,1)} async-done(((bf16[2,100,2048]{2,1,0:T(8,128)(2,1)}), bf16[32,100,2048]{2,1,0:T(8,128)(2,1)}) %all-gather.3.cloned.1.call-update) | async-done | bytes 13107216 | tf_op jit(solution)/shard_map/all_gather | solution.py:56
  93.9 22.6 %fusion.15 = (f32[32]{0:T(128)S(1)}, f32[2,32]{1,0:T(2,128)}) fusion(bf16[32,100,2048]{2,1,0:T(8,128)(2,1)} %all-gather.3.cloned.1.call-done, bf16[2,100,2048]{2,1,0:T(8,128)(2,1)} %fusion.6), kind=kOutput, calls=%fused_computation.22 | convolution fusion | flops 26214432 | bytes 13926784 | tf_op jit(solution)/shard_map/dot_general | solution.py:58
  116.5 3.8 %psum.35 = f32[32]{0:T(128)S(1)} all-reduce(f32[32]{0:T(128)S(1)} %get-tuple-element.5), channel_id=1, replica_groups=mesh['blk_0'=2,'blk_1'=4,'blk_2'=2,'walk_0'=2,'walk_1'=8] {'blk_0'}, use_global_device_ids=true, to_apply=%region_1.0 | all-reduce | flops 32 | bytes 256 | tf_op jit(solution)/shard_map/psum | solution.py:16
  120.3 8.4 %psum.36 = f32[32]{0:T(128)S(1)} all-reduce(f32[32]{0:T(128)S(1)} %psum.35), channel_id=1, replica_groups=mesh['blk_0'=2,'blk_1'=4,'blk_2'=2,'walk_0'=2,'walk_1'=8] {'blk_1'}, use_global_device_ids=true, to_apply=%region_2.0 | all-reduce | flops 32 | bytes 256 | tf_op jit(solution)/shard_map/psum | solution.py:16
  128.7 5.5 %psum.37 = f32[32]{0:T(128)S(1)} all-reduce(f32[32]{0:T(128)S(1)} %psum.36), channel_id=1, replica_groups=mesh['blk_0'=2,'blk_1'=4,'blk_2'=2,'walk_0'=2,'walk_1'=8] {'blk_2'}, use_global_device_ids=true, to_apply=%region_3.0 | all-reduce | flops 32 | bytes 256 | tf_op jit(solution)/shard_map/psum | solution.py:16
  134.2 5.3 %psum.38 = f32[32]{0:T(128)S(1)} all-reduce(f32[32]{0:T(128)S(1)} %psum.37), channel_id=1, replica_groups=mesh['blk_0'=2,'blk_1'=4,'blk_2'=2,'walk_0'=2,'walk_1'=8] {'walk_0'}, use_global_device_ids=true, to_apply=%region_4.0 | all-reduce | flops 32 | bytes 256 | tf_op jit(solution)/shard_map/psum | solution.py:16
  139.5 13.7 %psum.39 = f32[32]{0:T(128)S(1)} all-reduce(f32[32]{0:T(128)S(1)} %psum.38), channel_id=1, replica_groups=mesh['blk_0'=2,'blk_1'=4,'blk_2'=2,'walk_0'=2,'walk_1'=8] {'walk_1'}, use_global_device_ids=true, to_apply=%region_5.0 | all-reduce | flops 32 | bytes 256 | tf_op jit(solution)/shard_map/psum | solution.py:16
  153.2 0.0 copy-done.3
  153.2 0.5 fusion.14
  153.7 0.0 copy-done
  153.7 3.7 %fusion.10 = f32[1,128,2048]{2,0,1:T(1,128)S(1)} fusion(bf16[2,128,2048]{2,1,0:T(8,128)(2,1)S(1)} %copy-done, f32[32]{0:T(128)S(1)} %get-tuple-element.3, s32[]{:T(128)S(6)} %select_n.3), kind=kOutput, calls=%fused_computation.15 | convolution fusion | flops 6291456 | bytes 2097284 | tf_op jit(solution)/shard_map/dot_general | solution.py:66
  157.4 0.7 copy.25
  158.2 0.1 bitcast_multiply_fusion
  158.3 0.3 copy.21
  158.6 27.7 %all_to_all.10 = f32[16,128,128]{2,1,0:T(8,128)S(1)} all-to-all(f32[16,128,128]{2,1,0:T(8,128)S(1)} %copy.21), channel_id=1, replica_groups=mesh['blk_0'=2,'blk_1'=4,'blk_2'=2,'walk_0'=2,'walk_1'=8] {'walk_0','wal..., dimensions={0} | all-to-all | bytes 2097152 | tf_op jit(solution)/shard_map/all_to_all | solution.py:26
  186.3 0.1 reduce_sum.19
  186.4 0.1 copy.22
  186.5 0.1 broadcast_in_dim.2
  186.6 19.3 %all_to_all.11 = bf16[16,128,128]{1,2,0:T(8,128)(2,1)} all-to-all(bf16[16,128,128]{1,2,0:T(8,128)(2,1)S(1)} %broadcast_in_dim.2), channel_id=1, replica_groups=mesh['blk_0'=2,'blk_1'=4,'blk_2'=2,'walk_0'=2,'walk_1'=8] {'walk_0','wal..., dimensions={0} | all-to-all | bytes 1048576 | tf_op jit(solution)/shard_map/all_to_all | solution.py:32
  205.9 0.0 all-gather.5.cloned.1.call-update
  206.0 63.8 %all-gather.5.cloned.1.call-done = bf16[2048,2048]{0,1:T(8,128)(2,1)} async-done(((bf16[128,2048]{0,1:T(8,128)(2,1)}), bf16[2048,2048]{0,1:T(8,128)(2,1)}) %all-gather.5.cloned.1.call-update) | async-done | bytes 8388624 | tf_op jit(solution)/shard_map/all_gather | solution.py:71
  269.8 0.0 copy-start.4
  269.8 7.5 %convolution_convert_fusion = bf16[2048,400]{0,1:T(8,128)(2,1)S(1)} fusion(bf16[2048,2048]{0,1:T(8,128)(2,1)} %all-gather.5.cloned.1.call-done, bf16[400,2048]{1,0:T(8,128)(2,1)} %bitcast.41), kind=kOutput, calls=%fused_computation.10 | convolution fusion | flops 3356262400 | bytes 11665408 | tf_op jit(solution)/shard_map/dot_general | solution.py:75
  277.3 0.0 copy-done.4
  277.3 3.6 %multiply_convert_fusion.2 = bf16[400,2048]{1,0:T(8,128)(2,1)S(1)} fusion(bf16[2048,400]{0,1:T(8,128)(2,1)S(1)} %convolution_convert_fusion, bf16[2048,2048]{0,1:T(8,128)(2,1)S(1)} %copy-done.4), kind=kOutput, calls=%fused_computation.9 | convolution fusion | flops 3357081600 | bytes 11665408 | tf_op jit(solution)/shard_map/dot_general | solution.py:75
  280.9 0.0 copy-start.1
  281.0 3.6 %multiply_convert_fusion.1 = bf16[400,2048]{1,0:T(8,128)(2,1)S(1)} fusion(bf16[400,2048]{1,0:T(8,128)(2,1)S(1)} %multiply_convert_fusion.2, bf16[2048,2048]{0,1:T(8,128)(2,1)S(1)} %copy-done.4), kind=kOutput, calls=%fused_computation.8 | convolution fusion | flops 3357081600 | bytes 11665408 | tf_op jit(solution)/shard_map/dot_general | solution.py:75
  284.6 0.0 copy-done.1
  284.6 5.2 %fusion.5 = bf16[400,2048]{1,0:T(8,128)(2,1)} fusion(bf16[2048,400]{0,1:T(8,128)(2,1)S(1)} %convolution_convert_fusion, bf16[400,2048]{1,0:T(8,128)(2,1)S(1)} %multiply_convert_fusion.1, bf16[400,2048]{1,0:T(8,128)(2,1)S(1)} %multiply_convert_fusion.2, bf16[400,2048]{1,0:T(8,128)(2,1)S(1)} %bitcast.42, bf16[2048,2048]{0,1:T(8,128)(2,1)S(1)} %copy-done.4), kind=kOutput, calls=%fused_computation.6 | convolution fusion | flops 3365273600 | bytes 16580608 | tf_op jit(solution)/shard_map/dot_general | solution.py:75
Async XLA Ops:
  7.2 146.5 %copy-start = (bf16[2,128,2048]{2,1,0:T(8,128)(2,1)S(1)}, bf16[2,128,2048]{2,1,0:T(8,128)(2,1)}, u32[]{:S(2)}) copy-start(bf16[2,128,2048]{2,1,0:T(8,128)(2,1)} %param.8) | copy-start | bytes 3145732
  7.2 4.1 %copy-start.2 = (bf16[2,2,100,100]{3,1,2,0:T(2,128)(2,1)S(1)}, bf16[2,2,100,100]{3,1,2,0:T(2,128)(2,1)}, u32[]{:S(2)}) copy-start(bf16[2,2,100,100]{3,1,2,0:T(2,128)(2,1)} %param.6) | copy-start | bytes 240004
  7.2 86.7 %all-gather.3.cloned.1.call-start = ((), (), s32[]{:S(2)}) async-start(), calls=%async_computation.2 | async-start | bytes 14483456 | tf_op jit(solution)/shard_map/all_gather | solution.py:56
  9.7 260.1 %all-gather.5.cloned.1.call-start = ((), (), s32[]{:S(2)}) async-start(), calls=%async_computation.3 | async-start | bytes 8912896 | tf_op jit(solution)/shard_map/all_gather | solution.py:71
  12.7 140.5 %copy-start.3 = (f32[32]{0:T(128)S(1)}, f32[32]{0:T(128)}, u32[]{:S(2)}) copy-start(f32[32]{0:T(128)} %param.9) | copy-start | bytes 388
  269.8 7.6 %copy-start.4 = (bf16[2048,2048]{0,1:T(8,128)(2,1)S(1)}, bf16[2048,2048]{0,1:T(8,128)(2,1)}, u32[]{:S(2)}) copy-start(bf16[2048,2048]{0,1:T(8,128)(2,1)} %all-gather.5.cloned.1.call-done) | copy-start | bytes 25165828
  280.9 3.6 %copy-start.1 = (bf16[2,200,2048]{2,1,0:T(8,128)(2,1)S(1)}, bf16[2,200,2048]{2,1,0:T(8,128)(2,1)}, u32[]{:S(2)}) copy-start(bf16[2,200,2048]{2,1,0:T(8,128)(2,1)} %param.5) | copy-start | bytes 4915204
Sparse Core Ops, SparseCore 0:
  10.4 83.4 all-gather.2
  206.1 63.6 all-gather.4
where the time goes:
time: 297 us
  waiting for transfers between devices  145 us (49%)
  blocking collectives  83.7 us (28%)
  matrix products  47.6 us (16%)
  between operations  14.2 us (5%)
  local copies, waits for them, and re-layouts  5.29 us (2%)
    all_gather x1, waiting for transfers between devices, local(): piece = lax.all_gather(rotated_chol, BLK, axis=0, tiled=True)  81.3 us
    all_gather x1, waiting for transfers between devices, local(): field = lax.all_gather(row_block, BLK, axis=0, tiled=True)  63.8 us
    psum x5, blocking collectives, by_axis(): return functools.reduce(lax.psum, axes, array)  36.6 us
    all_to_all x1, blocking collectives, sent_and_summed(): lax.all_to_all(blocks, axis, split_axis=0, concat_axis=0, tiled=True)  27.7 us
    dot_general x1, matrix products, local(): lax.dot_general(flat_theta, flat_piece, (((1,), (1,)), ((), ())), preferr...  22.6 us
    dot_general x4, matrix products, local(): jnp.dot(current, field, preferred_element_type=jnp.float32) / order  19.9 us
    all_to_all x1, blocking collectives, sent_to_all(): lax.all_to_all(jnp.broadcast_to(array[None], (count, *array.shape)), axis...  19.3 us
  transfers between devices with their start and end apart: 2, of which 2 were waited for; matrix products, arithmetic and copies ran while one was open for 1% of the time, Pallas kernels for 0%

commit v1 on v0

--- a/solution.py
+++ b/solution.py
@@ -68,7 +68,9 @@
     )
     narrow = sent_and_summed(partial_value, WALK, 1).astype(jnp.bfloat16)
     row_block = gather_directly(narrow, WALK, 1)
-    field = lax.all_gather(row_block, BLK, axis=0, tiled=True)
+    field = jnp.concatenate(
+        lax.all_to_all(jnp.stack([row_block] * lax.axis_size(BLK)), BLK, 0, 0), axis=0
+    )
     current = walkers.reshape(wdev_count * double_rows, orbitals)
     total = current.astype(jnp.float32)
     for order in range(1, 5):

time: 297 us -> 334 us (1.12)
  blocking collectives: 83.7 us -> 187 us
  waiting for transfers between devices: 145 us -> 81.3 us
  matrix products: 47.6 us -> 43.6 us
    all_to_all x0 -> x1, blocking collectives: none -> 103 us  [local(): lax.all_to_all(jnp.stack([row_block] * lax.axis_size(BLK)), BLK, 0, 0)]
    all_gather x1 -> x0, waiting for transfers between devices: 63.8 us -> none  [local(): field = lax.all_gather(row_block, BLK, axis=0, tiled=True)]
    dot_general x4, matrix products: 19.9 us -> 15.9 us  [local(): jnp.dot(current, field, preferred_element_type=jnp.float32) / order]
  transfers between devices with their start and end apart: 2 -> 1, of which waited for: 2 -> 1; matrix products, arithmetic and copies ran while one was open for 1% -> 1% of each run, Pallas kernels for 0% -> 0%
where the time goes in v1:
time: 334 us; the launch traced here: 333 us
  blocking collectives  187 us (56%)
  waiting for transfers between devices  81.3 us (24%)
  matrix products  43.6 us (13%)
  between operations  14.2 us (4%)
  local copies, waits for them, and re-layouts  6.56 us (2%)
    all_to_all x1, blocking collectives, local(): lax.all_to_all(jnp.stack([row_block] * lax.axis_size(BLK)), BLK, 0, 0)  103 us
    all_gather x1, waiting for transfers between devices, local(): piece = lax.all_gather(rotated_chol, BLK, axis=0, tiled=True)  81.3 us
    psum x5, blocking collectives, by_axis(): return functools.reduce(lax.psum, axes, array)  36.6 us
    all_to_all x1, blocking collectives, sent_and_summed(): lax.all_to_all(blocks, axis, split_axis=0, concat_axis=0, tiled=True)  27.7 us
    dot_general x1, matrix products, local(): lax.dot_general(flat_theta, flat_piece, (((1,), (1,)), ((), ())), preferr...  22.6 us
    all_to_all x1, blocking collectives, sent_to_all(): lax.all_to_all(jnp.broadcast_to(array[None], (count, *array.shape)), axis...  19.2 us
    dot_general x4, matrix products, local(): jnp.dot(current, field, preferred_element_type=jnp.float32) / order  15.9 us
  transfers between devices with their start and end apart: 1, of which 1 were waited for; matrix products, arithmetic and copies ran while one was open for 1% of the time, Pallas kernels for 0%

profile of v1, /device:TPU:1, one launch (start us, length us, event | category | flops | bytes accessed | tf_op | source)
XLA Modules:
  0.0 333.2 jit_solution(5296502653791872378)
XLA Ops:
  7.2 0.0 copy-start
  7.2 0.0 copy-start.2
  7.2 0.0 all-gather.2.cloned.1.call-start
  7.2 2.4 copy.21
  9.6 0.0 all-gather.2.cloned.1.call-update
  9.7 1.6 reshape.29
  11.2 0.0 copy-done.2
  11.3 1.4 fusion.6
  12.6 0.0 copy-start.3
  12.6 81.3 %all-gather.2.cloned.1.call-done = bf16[32,100,2048]{2,1,0:T(8,128)(2,1)} async-done(((bf16[2,100,2048]{2,1,0:T(8,128)(2,1)}), bf16[32,100,2048]{2,1,0:T(8,128)(2,1)}) %all-gather.2.cloned.1.call-update) | async-done | bytes 13107216 | tf_op jit(solution)/shard_map/all_gather | solution.py:56
  93.9 22.6 %fusion.15 = (f32[32]{0:T(128)S(1)}, f32[2,32]{1,0:T(2,128)}) fusion(bf16[32,100,2048]{2,1,0:T(8,128)(2,1)} %all-gather.2.cloned.1.call-done, bf16[2,100,2048]{2,1,0:T(8,128)(2,1)} %fusion.6), kind=kOutput, calls=%fused_computation.22 | convolution fusion | flops 26214432 | bytes 13926784 | tf_op jit(solution)/shard_map/dot_general | solution.py:58
  116.5 3.8 %psum.35 = f32[32]{0:T(128)S(1)} all-reduce(f32[32]{0:T(128)S(1)} %get-tuple-element.5), channel_id=1, replica_groups=mesh['blk_0'=2,'blk_1'=4,'blk_2'=2,'walk_0'=2,'walk_1'=8] {'blk_0'}, use_global_device_ids=true, to_apply=%region_1.0 | all-reduce | flops 32 | bytes 256 | tf_op jit(solution)/shard_map/psum | solution.py:16
  120.3 8.4 %psum.36 = f32[32]{0:T(128)S(1)} all-reduce(f32[32]{0:T(128)S(1)} %psum.35), channel_id=1, replica_groups=mesh['blk_0'=2,'blk_1'=4,'blk_2'=2,'walk_0'=2,'walk_1'=8] {'blk_1'}, use_global_device_ids=true, to_apply=%region_2.0 | all-reduce | flops 32 | bytes 256 | tf_op jit(solution)/shard_map/psum | solution.py:16
  128.7 5.5 %psum.37 = f32[32]{0:T(128)S(1)} all-reduce(f32[32]{0:T(128)S(1)} %psum.36), channel_id=1, replica_groups=mesh['blk_0'=2,'blk_1'=4,'blk_2'=2,'walk_0'=2,'walk_1'=8] {'blk_2'}, use_global_device_ids=true, to_apply=%region_3.0 | all-reduce | flops 32 | bytes 256 | tf_op jit(solution)/shard_map/psum | solution.py:16
  134.2 5.3 %psum.38 = f32[32]{0:T(128)S(1)} all-reduce(f32[32]{0:T(128)S(1)} %psum.37), channel_id=1, replica_groups=mesh['blk_0'=2,'blk_1'=4,'blk_2'=2,'walk_0'=2,'walk_1'=8] {'walk_0'}, use_global_device_ids=true, to_apply=%region_4.0 | all-reduce | flops 32 | bytes 256 | tf_op jit(solution)/shard_map/psum | solution.py:16
  139.5 13.7 %psum.39 = f32[32]{0:T(128)S(1)} all-reduce(f32[32]{0:T(128)S(1)} %psum.38), channel_id=1, replica_groups=mesh['blk_0'=2,'blk_1'=4,'blk_2'=2,'walk_0'=2,'walk_1'=8] {'walk_1'}, use_global_device_ids=true, to_apply=%region_5.0 | all-reduce | flops 32 | bytes 256 | tf_op jit(solution)/shard_map/psum | solution.py:16
  153.2 0.0 copy-done.3
  153.2 0.5 fusion.14
  153.7 0.0 copy-done
  153.7 3.7 %fusion.10 = f32[1,128,2048]{2,0,1:T(1,128)S(1)} fusion(bf16[2,128,2048]{2,1,0:T(8,128)(2,1)S(1)} %copy-done, f32[32]{0:T(128)S(1)} %get-tuple-element.3, s32[]{:T(128)S(6)} %select_n.3), kind=kOutput, calls=%fused_computation.15 | convolution fusion | flops 6291456 | bytes 2097284 | tf_op jit(solution)/shard_map/dot_general | solution.py:66
  157.4 0.7 copy.29
  158.2 0.1 bitcast_multiply_fusion
  158.3 0.3 copy.24
  158.6 27.7 %all_to_all.15 = f32[16,128,128]{2,1,0:T(8,128)S(1)} all-to-all(f32[16,128,128]{2,1,0:T(8,128)S(1)} %copy.24), channel_id=1, replica_groups=mesh['blk_0'=2,'blk_1'=4,'blk_2'=2,'walk_0'=2,'walk_1'=8] {'walk_0','wal..., dimensions={0} | all-to-all | bytes 2097152 | tf_op jit(solution)/shard_map/all_to_all | solution.py:26
  186.3 0.1 reduce_sum.19
  186.4 0.1 copy.25
  186.5 0.1 broadcast_in_dim.2
  186.6 19.2 %all_to_all.16 = bf16[16,128,128]{1,2,0:T(8,128)(2,1)S(1)} all-to-all(bf16[16,128,128]{1,2,0:T(8,128)(2,1)S(1)} %broadcast_in_dim.2), channel_id=1, replica_groups=mesh['blk_0'=2,'blk_1'=4,'blk_2'=2,'walk_0'=2,'walk_1'=8] {'walk_0','wal..., dimensions={0} | all-to-all | bytes 1048576 | tf_op jit(solution)/shard_map/all_to_all | solution.py:32
  205.8 0.2 copy.26
  206.1 1.1 stack.3
  207.1 0.0 copy-start.1
  207.1 103.2 %all_to_all.17 = bf16[16,128,2048]{2,1,0:T(8,128)(2,1)S(1)} all-to-all(bf16[16,128,2048]{2,1,0:T(8,128)(2,1)S(1)} %stack.3), channel_id=1, replica_groups=mesh['blk_0'=2,'blk_1'=4,'blk_2'=2,'walk_0'=2,'walk_1'=8] {'blk_0','blk_..., dimensions={0} | all-to-all | bytes 16777216 | tf_op jit(solution)/shard_map/all_to_all | solution.py:72
  310.4 0.0 copy-done.1
  310.4 3.6 %convolution_convert_fusion = bf16[2048,400]{0,1:T(8,128)(2,1)S(1)} fusion(bf16[400,2048]{1,0:T(8,128)(2,1)S(1)} %bitcast.46, bf16[2048,2048]{1,0:T(8,128)(2,1)S(1)} %bitcast.40), kind=kOutput, calls=%fused_computation.10 | convolution fusion | flops 3356262400 | bytes 11665408 | tf_op jit(solution)/shard_map/dot_general | solution.py:77
  314.0 3.6 %multiply_convert_fusion.2 = bf16[400,2048]{1,0:T(8,128)(2,1)S(1)} fusion(bf16[2048,400]{0,1:T(8,128)(2,1)S(1)} %convolution_convert_fusion, bf16[2048,2048]{1,0:T(8,128)(2,1)S(1)} %bitcast.41), kind=kOutput, calls=%fused_computation.9 | convolution fusion | flops 3357081600 | bytes 11665408 | tf_op jit(solution)/shard_map/dot_general | solution.py:77
  317.6 3.6 %multiply_convert_fusion.1 = bf16[400,2048]{1,0:T(8,128)(2,1)S(1)} fusion(bf16[400,2048]{1,0:T(8,128)(2,1)S(1)} %multiply_convert_fusion.2, bf16[2048,2048]{1,0:T(8,128)(2,1)S(1)} %bitcast.42), kind=kOutput, calls=%fused_computation.8 | convolution fusion | flops 3357081600 | bytes 11665408 | tf_op jit(solution)/shard_map/dot_general | solution.py:77
  321.2 5.1 %fusion.5 = bf16[400,2048]{1,0:T(8,128)(2,1)} fusion(bf16[2048,400]{0,1:T(8,128)(2,1)S(1)} %convolution_convert_fusion, bf16[400,2048]{1,0:T(8,128)(2,1)S(1)} %multiply_convert_fusion.1, bf16[400,2048]{1,0:T(8,128)(2,1)S(1)} %multiply_convert_fusion.2, bf16[400,2048]{1,0:T(8,128)(2,1)S(1)} %bitcast.47, bf16[2048,2048]{1,0:T(8,128)(2,1)S(1)} %bitcast.43), kind=kOutput, calls=%fused_computation.6 | convolution fusion | flops 3365273600 | bytes 16580608 | tf_op jit(solution)/shard_map/dot_general | solution.py:77
Async XLA Ops:
  7.2 146.5 %copy-start = (bf16[2,128,2048]{2,1,0:T(8,128)(2,1)S(1)}, bf16[2,128,2048]{2,1,0:T(8,128)(2,1)}, u32[]{:S(2)}) copy-start(bf16[2,128,2048]{2,1,0:T(8,128)(2,1)} %param.8) | copy-start | bytes 3145732
  7.2 4.1 %copy-start.2 = (bf16[2,2,100,100]{3,1,2,0:T(2,128)(2,1)S(1)}, bf16[2,2,100,100]{3,1,2,0:T(2,128)(2,1)}, u32[]{:S(2)}) copy-start(bf16[2,2,100,100]{3,1,2,0:T(2,128)(2,1)} %param.6) | copy-start | bytes 240004
  7.2 86.7 %all-gather.2.cloned.1.call-start = ((), (), s32[]{:S(2)}) async-start(), calls=%async_computation.3 | async-start | bytes 14483456 | tf_op jit(solution)/shard_map/all_gather | solution.py:56
  12.6 140.6 %copy-start.3 = (f32[32]{0:T(128)S(1)}, f32[32]{0:T(128)}, u32[]{:S(2)}) copy-start(f32[32]{0:T(128)} %param.9) | copy-start | bytes 388
  207.1 103.2 %copy-start.1 = (bf16[2,200,2048]{2,1,0:T(8,128)(2,1)S(1)}, bf16[2,200,2048]{2,1,0:T(8,128)(2,1)}, u32[]{:S(2)}) copy-start(bf16[2,200,2048]{2,1,0:T(8,128)(2,1)} %param.5) | copy-start | bytes 4915204
Sparse Core Ops, SparseCore 0:
  10.4 83.4 all-gather.1
